TPU v7x, 32 devices: a whole 2x2x4 slice. The times are simulated.
32 devices in a mesh: ctx: 4 (over y, x), head: 8 (over z, core).
Axes of the slice: x: 2, y: 2, z: 4, core: 2. Of those that a mesh axis runs over, the one named last changes fastest.
Arguments:
- queries: bfloat16 [512, 3072], P('ctx', 'head'), may hold values from -10 to 10
- latent: bfloat16 [512, 576], P('ctx'), may hold values from -10 to 10
- block_of: int32 [8], replicated, may hold values from 0 to 7, each once
- key_up: bfloat16 [16, 128, 512], P('head'), may hold values from -0.5 to 0.5
- value_up: bfloat16 [16, 512, 128], P('head'), may hold values from -0.25 to 0.25
- out_grad: bfloat16 [512, 2048], P('ctx', 'head'), may hold values from -6 to 6
Outputs:
- attended: bfloat16 [512, 2048], P('ctx', 'head')
- query_grad: bfloat16 [512, 3072], P('ctx', 'head')
- latent_grad: float32 [512, 576], P('ctx')
Inputs may be any that keep to these rules, and one draw needn't show every extreme that they name: `block_of`: a permutation of the 8 blocks.
All inputs are finite; a program needn't handle non-finite values.
Results may differ from a plain program's by a relative error of at most 0.0099.
Values may be sent and summed in bfloat16 or wider, within the bound.
No kernel may reach another device: no remote copies, remote signals or barrier semaphores. Data moves between devices by JAX's collectives and lax.ppermute only.
A program may use at most 64 MiB of HBM per device.

v0:
```python
import math
import jax
import jax.numpy as jnp
from jax import lax
from jax.sharding import PartitionSpec as P

BLK_DEV = 2


def on_device(queries, latent, block_of, key_up, value_up, out_grad):
    local_rows = queries.shape[0]
    head_count = key_up.shape[0]
    nope_width = key_up.shape[1]
    latent_width = key_up.shape[2]
    joined_width = latent.shape[1]
    rope_width = joined_width - latent_width
    value_width = value_up.shape[2]
    score_scale = 1.0 / math.sqrt(nope_width + rope_width)
    all_latent = lax.all_gather(latent, "ctx", axis=0, tiled=True)
    total_rows = all_latent.shape[0]
    block_rows = local_rows // BLK_DEV
    row_index = jnp.arange(total_rows, dtype=jnp.int32)
    owner = (row_index // block_rows)[:, None] == jnp.arange(block_of.shape[0], dtype=jnp.int32)[
        None, :
    ]
    all_positions = (
        jnp.sum(jnp.where(owner, block_of[None, :], 0), axis=1) * block_rows
        + row_index % block_rows
    )
    my_positions = lax.dynamic_slice_in_dim(
        all_positions, lax.axis_index("ctx") * local_rows, local_rows
    )
    visible = all_positions[None, :] <= my_positions[:, None]
    query_heads = jnp.transpose(
        queries.reshape(local_rows, head_count, nope_width + rope_width), (1, 0, 2)
    )
    q_latent = jnp.einsum(
        "htn,hnl->htl", query_heads[:, :, :nope_width], key_up, preferred_element_type=jnp.float32
    ).astype(jnp.bfloat16)
    q_joined = jnp.concatenate([q_latent, query_heads[:, :, nope_width:]], axis=2)
    scores = (
        jnp.einsum("htw,kw->htk", q_joined, all_latent, preferred_element_type=jnp.float32)
        * score_scale
    )
    scores = jnp.where(visible[None], scores, -1e30)
    row_max = jnp.max(scores, axis=2, keepdims=True)
    expo = jnp.exp(scores - row_max)
    probs = expo / jnp.sum(expo, axis=2, keepdims=True)
    probs_low = probs.astype(jnp.bfloat16)
    latent_part = all_latent[:, :latent_width]
    out_latent = jnp.einsum(
        "htk,kl->htl", probs_low, latent_part, preferred_element_type=jnp.float32
    ).astype(jnp.bfloat16)
    attended = jnp.einsum(
        "htl,hlv->htv", out_latent, value_up, preferred_element_type=jnp.float32
    ).astype(jnp.bfloat16)
    attended = jnp.transpose(attended, (1, 0, 2)).reshape(local_rows, head_count * value_width)
    grad_heads = jnp.transpose(out_grad.reshape(local_rows, head_count, value_width), (1, 0, 2))
    grad_latent = jnp.einsum(
        "htv,hlv->htl", grad_heads, value_up, preferred_element_type=jnp.float32
    ).astype(jnp.bfloat16)
    grad_probs = jnp.einsum(
        "htl,kl->htk", grad_latent, latent_part, preferred_element_type=jnp.float32
    )
    delta = jnp.sum(probs * grad_probs, axis=2, keepdims=True)
    grad_scores = (probs * (grad_probs - delta) * score_scale).astype(jnp.bfloat16)
    grad_joined = jnp.einsum(
        "htk,kw->htw", grad_scores, all_latent, preferred_element_type=jnp.float32
    )
    grad_nope = jnp.einsum(
        "htl,hnl->htn",
        grad_joined[:, :, :latent_width].astype(jnp.bfloat16),
        key_up,
        preferred_element_type=jnp.float32,
    ).astype(jnp.bfloat16)
    grad_query = jnp.concatenate(
        [grad_nope, grad_joined[:, :, latent_width:].astype(jnp.bfloat16)], axis=2
    )
    query_grad = jnp.transpose(grad_query, (1, 0, 2)).reshape(
        local_rows, head_count * (nope_width + rope_width)
    )
    key_terms = jnp.einsum("htk,htw->kw", grad_scores, q_joined, preferred_element_type=jnp.float32)
    value_terms = jnp.einsum(
        "htk,htl->kl", probs_low, grad_latent, preferred_element_type=jnp.float32
    )
    key_terms = key_terms + jnp.pad(value_terms, ((0, 0), (0, rope_width)))
    columns = lax.psum_scatter(key_terms, "head", scatter_dimension=1, tiled=True)
    owned = lax.psum_scatter(columns, "ctx", scatter_dimension=0, tiled=True)
    latent_grad = lax.all_gather(owned, "head", axis=1, tiled=True)
    return (attended, query_grad, latent_grad)


def solution(mesh):
    return jax.shard_map(
        on_device,
        mesh=mesh,
        in_specs=(
            P("ctx", "head"),
            P("ctx", None),
            P(),
            P("head", None, None),
            P("head", None, None),
            P("ctx", "head"),
        ),
        out_specs=(P("ctx", "head"), P("ctx", "head"), P("ctx", None)),
        check_vma=False,
    )
```

profile of v0, /device:TPU:0, one launch (start us, length us, event | category | flops | bytes accessed | tf_op | source)
XLA Modules:
  0.0 109.3 jit_solution(8177717170956661955)
XLA Ops:
  7.2 0.0 copy-start
  7.2 0.0 copy-start.2
  7.2 0.0 copy-start.3
  7.2 0.0 reduce-scatter.3.cloned.1.call-start
  7.3 0.8 select_reduce_fusion
  8.1 0.1 dynamic_slice.3
  8.1 0.1 broadcast_compare_fusion
  8.3 1.0 copy.29
  9.3 0.1 copy.30
  9.4 1.2 %convolution_convert_fusion.3 = bf16[2,128,512]{2,1,0:T(8,128)(2,1)S(1)} fusion(bf16[2,128,512]{2,1,0:T(8,128)(2,1)} %param.9, bf16[2,128,192]{2,1,0:T(8,128)(2,1)S(1)} %bitcast.45), kind=kOutput, calls=%fused_computation.16 | convolution fusion | flops 33685504 | bytes 589824 | tf_op jit(solution)/shard_map/htn,hnl->htl/dot_general | solution.py:37
  10.6 0.0 copy-done.2
  10.6 11.8 %all_gather.6 = bf16[512,576]{0,1:T(8,128)(2,1)S(1)} all-gather(bf16[128,576]{0,1:T(8,128)(2,1)S(1)} %copy-done.2), channel_id=1, replica_groups=mesh['ctx'=4,'head'=8] {'ctx'}, dimensions={0}, use_global_device_ids=true | all-gather | bytes 737280 | tf_op jit(solution)/shard_map/all_gather | solution.py:19
  22.4 0.0 copy-done
  22.4 0.0 copy-done.3
  22.4 0.2 convolution_convert_fusion.1
  22.6 0.3 fusion.18
  22.9 0.4 fusion.5
  23.3 0.4 fusion.41
  23.8 1.7 %convolution_bitcast_fusion.1 = f32[512,512]{0,1:T(8,128)} fusion(bf16[2,128,512]{2,1,0:T(8,128)(2,1)S(1)} %convolution_convert_fusion.1, f32[2,128]{1,0:T(2,128)S(1)} %get-tuple-element.12, f32[2,128,512]{2,1,0:T(8,128)S(1)} %fusion.5), kind=kOutput, calls=%fused_computation.3 | convolution fusion | flops 134611712 | bytes 1836032 | tf_op jit(solution)/shard_map/htk,htl->kl/dot_general | solution.py:83
  25.5 3.6 %fusion.2 = f32[512,576]{0,1:T(8,128)} fusion(f32[512,512]{0,1:T(8,128)} %convolution_bitcast_fusion.1, f32[2,128,512]{2,1,0:T(8,128)S(1)} %fusion.18, bf16[2,128,64]{2,1,0:T(8,128)(2,1)S(1)} %slice.23, bf16[2,128,512]{2,1,0:T(8,128)(2,1)S(1)} %convolution_convert_fusion.3, f32[2,128,512]{2,1,0:T(8,128)S(1)} %get-tuple-element.13, ...), kind=kOutput, calls=%fused_computation.4 | convolution fusion | flops 152797952 | bytes 3572736 | tf_op jit(solution)/shard_map/htk,htw->kw/dot_general | solution.py:82
  29.1 0.0 reduce-scatter.3.cloned.1.call-update
  29.1 0.0 reduce-scatter.5.cloned.1.call-start
  29.2 0.9 fusion.11
  30.1 0.7 copy.39
  30.8 0.0 copy-start.1
  30.8 0.9 convolution_convert_fusion
  31.7 30.9 %reduce-scatter.3.cloned.1.call-done = f32[512,72]{0,1:T(8,128)} async-done(((f32[512,576]{0,1:T(8,128)}), f32[512,72]{0,1:T(8,128)}) %reduce-scatter.3.cloned.1.call-update) | async-done | bytes 147472 | tf_op jit(solution)/shard_map/reduce_scatter | solution.py:87
  62.6 0.0 reduce-scatter.5.cloned.1.call-update
  62.6 0.0 copy-done.1
  62.6 0.2 convolution_convert_fusion.4
  62.8 0.8 copy.40
  63.6 23.6 %reduce-scatter.5.cloned.1.call-done = f32[128,72]{0,1:T(8,128)} async-done(((f32[512,72]{0,1:T(8,128)}), f32[128,72]{0,1:T(8,128)}) %reduce-scatter.5.cloned.1.call-update) | async-done | bytes 36880 | tf_op jit(solution)/shard_map/reduce_scatter | solution.py:88
  87.2 14.6 %all_gather.7 = f32[128,576]{0,1:T(8,128)S(1)} all-gather(f32[128,72]{0,1:T(8,128)} %reduce-scatter.5.cloned.1.call-done), channel_id=1, replica_groups=mesh['ctx'=4,'head'=8] {'head'}, dimensions={1}, use_global_device_ids=true | all-gather | bytes 331776 | tf_op jit(solution)/shard_map/all_gather | solution.py:89
  101.7 0.7 copy.56
  (5 shorter events, 0.0 us)
Async XLA Ops:
  7.2 15.2 %copy-start = (bf16[2,512,128]{2,1,0:T(8,128)(2,1)S(1)}, bf16[2,512,128]{2,1,0:T(8,128)(2,1)}, u32[]{:S(2)}) copy-start(bf16[2,512,128]{2,1,0:T(8,128)(2,1)} %param.10) | copy-start | bytes 786436
  7.2 3.4 %copy-start.2 = (bf16[128,576]{0,1:T(8,128)(2,1)S(1)}, bf16[128,576]{0,1:T(8,128)(2,1)}, u32[]{:S(2)}) copy-start(bf16[128,576]{0,1:T(8,128)(2,1)} %param.7) | copy-start | bytes 442372
  7.2 15.2 %copy-start.3 = (bf16[128,256]{1,0:T(8,128)(2,1)S(1)}, bf16[128,256]{1,0:T(8,128)(2,1)}, u32[]{:S(2)}) copy-start(bf16[128,256]{1,0:T(8,128)(2,1)} %param.11) | copy-start | bytes 196612
  7.2 55.4 %reduce-scatter.3.cloned.1.call-start = ((), (), s32[]{:S(2)}) async-start(), calls=%async_computation.2 | async-start | bytes 1327104 | tf_op jit(solution)/shard_map/reduce_scatter | solution.py:87
  29.1 58.0 %reduce-scatter.5.cloned.1.call-start = ((), (), s32[]{:S(2)}) async-start(), calls=%async_computation.3 | async-start | bytes 184320 | tf_op jit(solution)/shard_map/reduce_scatter | solution.py:88
  30.8 31.8 %copy-start.1 = (bf16[2,128,512]{2,1,0:T(8,128)(2,1)S(1)}, bf16[2,128,512]{2,1,0:T(8,128)(2,1)}, u32[]{:S(2)}) copy-start(bf16[2,128,512]{2,1,0:T(8,128)(2,1)} %param.9) | copy-start | bytes 786436
Sparse Core Ops, SparseCore 0:
  29.3 33.2 reduce-scatter.2
  65.3 21.8 reduce-scatter.4
where the time goes:
time: 110 us; the launch traced here: 109 us
  waiting for transfers between devices  54.5 us (50%)
  blocking collectives  26.4 us (24%)
  between operations  14.2 us (13%)
  matrix products  9.4 us (9%)
  local copies, waits for them, and re-layouts  3.44 us (3%)
  other arithmetic  1.35 us (1%)
    reduce_scatter x1, waiting for transfers between devices, on_device(): lax.psum_scatter(key_terms, 'head', scatter_dimension=1, tiled=True)  30.9 us
    reduce_scatter x1, waiting for transfers between devices, on_device(): owned = lax.psum_scatter(columns, 'ctx', scatter_dimension=0, tiled=True)  23.6 us
    all_gather x1, blocking collectives, on_device(): latent_grad = lax.all_gather(owned, 'head', axis=1, tiled=True)  14.6 us
    all_gather x1, blocking collectives, on_device(): all_latent = lax.all_gather(latent, 'ctx', axis=0, tiled=True)  11.8 us
    dot_general x1, matrix products, on_device(): jnp.einsum('htk,htw->kw', grad_scores, q_joined, preferred_element_type=j...  3.62 us
    unnamed x12, local copies, waits for them, and re-layouts  3.24 us
  transfers between devices with their start and end apart: 2, of which 2 were waited for; matrix products, arithmetic and copies ran while one was open for 3% of the time, Pallas kernels for 0%

commit v1 on v0

--- a/solution.py
+++ b/solution.py
@@ -5,6 +5,28 @@
 from jax.sharding import PartitionSpec as P
 
 BLK_DEV = 2
+
+
+def in_order(pieces, dim):
+    lengths = list(pieces.shape[1:])
+    lengths[dim] *= pieces.shape[0]
+    return jnp.moveaxis(pieces, 0, dim).reshape(lengths)
+
+
+def collect(array, axis, dim):
+    size = lax.axis_size(axis)
+    pairs = [(i, (i + 1) % size) for i in range(size)]
+    back = [(b, a) for a, b in pairs]
+    lower, upper = ([], [])
+    for lap in range(size - 1):
+        if lap % 2 == 0:
+            lower.append(lax.ppermute(lower[-1] if lower else array, axis, pairs))
+        else:
+            upper.append(lax.ppermute(upper[-1] if upper else array, axis, back))
+    parts = jnp.stack([*lower[::-1], array, *upper])
+    shift = lax.axis_index(axis) - len(lower)
+    parts = parts[(jnp.arange(size) - shift) % size]
+    return in_order(parts, dim)
 
 
 def on_device(queries, latent, block_of, key_up, value_up, out_grad):
@@ -86,7 +108,7 @@
     key_terms = key_terms + jnp.pad(value_terms, ((0, 0), (0, rope_width)))
     columns = lax.psum_scatter(key_terms, "head", scatter_dimension=1, tiled=True)
     owned = lax.psum_scatter(columns, "ctx", scatter_dimension=0, tiled=True)
-    latent_grad = lax.all_gather(owned, "head", axis=1, tiled=True)
+    latent_grad = collect(owned, "head", 1)
     return (attended, query_grad, latent_grad)
 
 

time: 110 us -> 118 us (1.073)
  blocking collectives: 26.4 us -> 12.4 us
  waiting for transfers between devices: 54.5 us -> 66.3 us
  starting transfers between devices: 0.08 us -> 10.6 us
    all_gather x1 -> x0, blocking collectives: 14.6 us -> none  [on_device(): latent_grad = lax.all_gather(owned, 'head', axis=1, tiled=True)]
    ppermute x0 -> x7, starting transfers between devices: none -> 10.6 us  [the longest x3 10.6 us: collect(): upper.append(lax.ppermute(upper[-1] if upper else array, axis, back))]
    ppermute x0 -> x7, waiting for transfers between devices: none -> 10.1 us  [the longest x4 8.38 us: collect(): lower.append(lax.ppermute(lower[-1] if lower else array, axis, pairs))]
    reduce_scatter x1, waiting for transfers between devices: 30.9 us -> 33.3 us  [on_device(): lax.psum_scatter(key_terms, 'head', scatter_dimension=1, tiled=True)]
    gather x0 -> x1, local copies, waits for them, and re-layouts: none -> 1.28 us  [collect(): parts = parts[(jnp.arange(size) - shift) % size]]
    unnamed x12 -> x18, local copies, waits for them, and re-layouts: 3.24 us -> 2.56 us
  transfers between devices with their start and end apart: 2 -> 9, of which waited for: 2 -> 8; matrix products, arithmetic and copies ran while one was open for 3% -> 3% of each run, Pallas kernels for 0% -> 0%
where the time goes in v1:
time: 118 us; the launch traced here: 117 us
  waiting for transfers between devices  66.3 us (56%)
  between operations  14.3 us (12%)
  blocking collectives  12.4 us (11%)
  starting transfers between devices  10.6 us (9%)
  matrix products  8.45 us (7%)
  local copies, waits for them, and re-layouts  4.04 us (3%)
  other arithmetic  1.31 us (1%)
    reduce_scatter x1, waiting for transfers between devices, on_device(): lax.psum_scatter(key_terms, 'head', scatter_dimension=1, tiled=True)  33.3 us
    reduce_scatter x1, waiting for transfers between devices, on_device(): owned = lax.psum_scatter(columns, 'ctx', scatter_dimension=0, tiled=True)  23 us
    all_gather x1, blocking collectives, on_device(): all_latent = lax.all_gather(latent, 'ctx', axis=0, tiled=True)  12.4 us
    ppermute x3, starting transfers between devices, collect(): upper.append(lax.ppermute(upper[-1] if upper else array, axis, back))  10.6 us
    ppermute x4, waiting for transfers between devices, collect(): lower.append(lax.ppermute(lower[-1] if lower else array, axis, pairs))  8.38 us
    dot_general x1, matrix products, on_device(): jnp.einsum('htk,htw->kw', grad_scores, q_joined, preferred_element_type=j...  3.62 us
    unnamed x18, local copies, waits for them, and re-layouts  2.56 us
  transfers between devices with their start and end apart: 9, of which 8 were waited for; matrix products, arithmetic and copies ran while one was open for 3% of the time, Pallas kernels for 0%

profile of v1, /device:TPU:0, one launch (start us, length us, event | category | flops | bytes accessed | tf_op | source)
XLA Modules:
  0.0 117.5 jit_solution(4114440800176025798)
XLA Ops:
  7.2 0.0 copy-start
  7.2 0.0 copy-start.1
  7.2 0.0 reduce-scatter.3.cloned.1.call-start
  7.2 12.4 %all_gather.3 = bf16[512,576]{0,1:T(8,128)(2,1)S(1)} all-gather(bf16[128,576]{0,1:T(8,128)(2,1)} %param.7), channel_id=1, replica_groups=mesh['ctx'=4,'head'=8] {'ctx'}, dimensions={0}, use_global_device_ids=true | all-gather | bytes 737280 | tf_op jit(solution)/shard_map/all_gather | solution.py:41
  19.7 0.7 select_reduce_fusion
  20.4 0.1 dynamic_slice.3
  20.5 0.1 broadcast_compare_fusion
  20.6 1.0 copy.29
  21.6 0.1 copy.30
  21.8 0.0 copy-done.1
  21.8 0.2 convolution_convert_fusion.3
  22.0 0.0 copy-start.2
  22.0 0.4 fusion.5
  22.4 0.4 fusion.43
  22.8 0.0 copy-done
  22.8 0.0 copy-done.2
  22.8 0.2 convolution_convert_fusion.1
  23.1 0.3 fusion.18
  23.4 1.7 %convolution_bitcast_fusion.1 = f32[512,512]{0,1:T(8,128)} fusion(bf16[2,128,512]{2,1,0:T(8,128)(2,1)S(1)} %convolution_convert_fusion.1, f32[2,128]{1,0:T(2,128)S(1)} %get-tuple-element.12, f32[2,128,512]{2,1,0:T(8,128)S(1)} %fusion.5), kind=kOutput, calls=%fused_computation.4 | convolution fusion | flops 134611712 | bytes 1836032 | tf_op jit(solution)/shard_map/htk,htl->kl/dot_general | solution.py:105
  25.1 3.6 %fusion.2 = f32[512,576]{0,1:T(8,128)} fusion(f32[512,512]{0,1:T(8,128)} %convolution_bitcast_fusion.1, f32[2,128,512]{2,1,0:T(8,128)S(1)} %fusion.18, bf16[2,128,64]{2,1,0:T(8,128)(2,1)S(1)} %slice.25, bf16[2,128,512]{2,1,0:T(8,128)(2,1)S(1)} %convolution_convert_fusion.3, f32[2,128,512]{2,1,0:T(8,128)S(1)} %get-tuple-element.13, ...), kind=kOutput, calls=%fused_computation.5 | convolution fusion | flops 152797952 | bytes 3572736 | tf_op jit(solution)/shard_map/htk,htw->kw/dot_general | solution.py:104
  28.8 0.0 reduce-scatter.3.cloned.1.call-update
  28.8 0.0 reduce-scatter.5.cloned.1.call-start
  28.8 33.3 %reduce-scatter.3.cloned.1.call-done = f32[512,72]{0,1:T(8,128)} async-done(((f32[512,576]{0,1:T(8,128)}), f32[512,72]{0,1:T(8,128)}) %reduce-scatter.3.cloned.1.call-update) | async-done | bytes 147472 | tf_op jit(solution)/shard_map/reduce_scatter | solution.py:109
  62.1 0.0 reduce-scatter.5.cloned.1.call-update
  62.1 0.9 fusion.11
  63.0 0.9 convolution_convert_fusion
  63.9 23.0 %reduce-scatter.5.cloned.1.call-done = f32[128,72]{0,1:T(8,128)} async-done(((f32[512,72]{0,1:T(8,128)}), f32[128,72]{0,1:T(8,128)}) %reduce-scatter.5.cloned.1.call-update) | async-done | bytes 36880 | tf_op jit(solution)/shard_map/reduce_scatter | solution.py:110
  86.8 0.0 copy-start.3
  86.8 0.0 collective-permute-start
  86.8 0.2 convolution_convert_fusion.4
  87.1 5.2 %collective-permute-done = f32[128,72]{0,1:T(8,128)S(1)} collective-permute-done((f32[128,72]{0,1:T(8,128)}, f32[128,72]{0,1:T(8,128)S(1)}, u32[]{:S(2)}, u32[]{:S(2)}) %collective-permute-start) | collective-permute-done | bytes 36896 | tf_op jit(solution)/shard_map/ppermute | solution.py:23
  92.2 0.0 collective-permute-start.1
  92.3 3.6 %collective-permute-start.4 = (f32[128,72]{0,1:T(8,128)}, f32[128,72]{0,1:T(8,128)S(1)}, u32[]{:S(2)}, u32[]{:S(2)}) collective-permute-start(f32[128,72]{0,1:T(8,128)} %reduce-scatter.5.cloned.1.call-done), channel_id=1, source_target_pairs={{1,0},{2,1},{3,2},{4,3},{5,4},{6,5},{7,6},{0,7},{9,8},{10,9},{11,1... | collective-permute-start | bytes 110600 | tf_op jit(solution)/shard_map/ppermute | solution.py:25
  95.8 1.7 %collective-permute-done.1 = f32[128,72]{0,1:T(8,128)S(1)} collective-permute-done((f32[128,72]{0,1:T(8,128)S(1)}, f32[128,72]{0,1:T(8,128)S(1)}, u32[]{:S(2)}, u32[]{:S(2)}) %collective-permute-start.1) | collective-permute-done | bytes 36896 | tf_op jit(solution)/shard_map/ppermute | solution.py:23
  97.5 0.0 collective-permute-start.2
  97.5 0.3 collective-permute-done.4
  97.8 3.4 %collective-permute-start.5 = (f32[128,72]{0,1:T(8,128)S(1)}, f32[128,72]{0,1:T(8,128)S(1)}, u32[]{:S(2)}, u32[]{:S(2)}) collective-permute-start(f32[128,72]{0,1:T(8,128)S(1)} %collective-permute-done.4), channel_id=1, source_target_pairs={{1,0},{2,1},{3,2},{4,3},{5,4},{6,5},{7,6},{0,7},{9,8},{10,9},{11,1... | collective-permute-start | bytes 110600 | tf_op jit(solution)/shard_map/ppermute | solution.py:25
  101.2 1.4 %collective-permute-done.2 = f32[128,72]{0,1:T(8,128)S(1)} collective-permute-done((f32[128,72]{0,1:T(8,128)S(1)}, f32[128,72]{0,1:T(8,128)S(1)}, u32[]{:S(2)}, u32[]{:S(2)}) %collective-permute-start.2) | collective-permute-done | bytes 36896 | tf_op jit(solution)/shard_map/ppermute | solution.py:23
  102.7 0.0 collective-permute-start.3
  102.7 0.7 copy.39
  103.4 0.8 copy.40
  104.2 0.0 collective-permute-done.5
  104.2 3.5 %collective-permute-start.6 = (f32[128,72]{0,1:T(8,128)S(1)}, f32[128,72]{0,1:T(8,128)S(1)}, u32[]{:S(2)}, u32[]{:S(2)}) collective-permute-start(f32[128,72]{0,1:T(8,128)S(1)} %collective-permute-done.5), channel_id=1, source_target_pairs={{1,0},{2,1},{3,2},{4,3},{5,4},{6,5},{7,6},{0,7},{9,8},{10,9},{11,1... | collective-permute-start | bytes 110600 | tf_op jit(solution)/shard_map/ppermute | solution.py:25
  107.7 0.1 collective-permute-done.3
  107.9 0.0 copy-done.3
  107.9 1.4 %collective-permute-done.6 = f32[128,72]{0,1:T(8,128)S(1)} collective-permute-done((f32[128,72]{0,1:T(8,128)S(1)}, f32[128,72]{0,1:T(8,128)S(1)}, u32[]{:S(2)}, u32[]{:S(2)}) %collective-permute-start.6) | collective-permute-done | bytes 36896 | tf_op jit(solution)/shard_map/ppermute | solution.py:25
  109.4 1.3 %gather_fusion = f32[8,128,72]{1,2,0:T(8,128)} fusion(f32[8,128,72]{1,2,0:T(8,128)S(1)} %bitcast_dynamic-update-slice_fusion, s32[1024]{0:T(1024)S(1)} %pad_clamp_fusion), kind=kCustom, calls=%fused_computation | custom fusion | bytes 589856 | tf_op jit(solution)/shard_map/gather | solution.py:28
  (15 shorter events, 0.1 us)
Async XLA Ops:
  7.2 15.7 %copy-start = (bf16[2,512,128]{2,1,0:T(8,128)(2,1)S(1)}, bf16[2,512,128]{2,1,0:T(8,128)(2,1)}, u32[]{:S(2)}) copy-start(bf16[2,512,128]{2,1,0:T(8,128)(2,1)} %param.10) | copy-start | bytes 786436
  7.2 14.6 %copy-start.1 = (bf16[2,128,512]{2,1,0:T(8,128)(2,1)S(1)}, bf16[2,128,512]{2,1,0:T(8,128)(2,1)}, u32[]{:S(2)}) copy-start(bf16[2,128,512]{2,1,0:T(8,128)(2,1)} %param.9) | copy-start | bytes 786436
  7.2 54.9 %reduce-scatter.3.cloned.1.call-start = ((), (), s32[]{:S(2)}) async-start(), calls=%async_computation.2 | async-start | bytes 1327104 | tf_op jit(solution)/shard_map/reduce_scatter | solution.py:109
  22.0 0.8 copy-start.2
  28.8 58.1 %reduce-scatter.5.cloned.1.call-start = ((), (), s32[]{:S(2)}) async-start(), calls=%async_computation.3 | async-start | bytes 184320 | tf_op jit(solution)/shard_map/reduce_scatter | solution.py:110
  86.8 21.1 %copy-start.3 = (f32[128,72]{0,1:T(8,128)S(1)}, f32[128,72]{0,1:T(8,128)}, u32[]{:S(2)}) copy-start(f32[128,72]{0,1:T(8,128)} %reduce-scatter.5.cloned.1.call-done) | copy-start | bytes 110596
  86.8 5.4 %collective-permute-start = (f32[128,72]{0,1:T(8,128)}, f32[128,72]{0,1:T(8,128)S(1)}, u32[]{:S(2)}, u32[]{:S(2)}) collective-permute-start(f32[128,72]{0,1:T(8,128)} %reduce-scatter.5.cloned.1.call-done), channel_id=1, source_target_pairs={{0,1},{1,2},{2,3},{3,4},{4,5},{5,6},{6,7},{7,0},{8,9},{9,10},{10,1... | collective-permute-start | bytes 110600 | tf_op jit(solution)/shard_map/ppermute | solution.py:23
  92.2 5.3 %collective-permute-start.1 = (f32[128,72]{0,1:T(8,128)S(1)}, f32[128,72]{0,1:T(8,128)S(1)}, u32[]{:S(2)}, u32[]{:S(2)}) collective-permute-start(f32[128,72]{0,1:T(8,128)S(1)} %collective-permute-done), channel_id=1, source_target_pairs={{0,1},{1,2},{2,3},{3,4},{4,5},{5,6},{6,7},{7,0},{8,9},{9,10},{10,1... | collective-permute-start | bytes 110600 | tf_op jit(solution)/shard_map/ppermute | solution.py:23
  92.3 5.5 %collective-permute-start.4 = (f32[128,72]{0,1:T(8,128)}, f32[128,72]{0,1:T(8,128)S(1)}, u32[]{:S(2)}, u32[]{:S(2)}) collective-permute-start(f32[128,72]{0,1:T(8,128)} %reduce-scatter.5.cloned.1.call-done), channel_id=1, source_target_pairs={{1,0},{2,1},{3,2},{4,3},{5,4},{6,5},{7,6},{0,7},{9,8},{10,9},{11,1... | collective-permute-start | bytes 110600 | tf_op jit(solution)/shard_map/ppermute | solution.py:25
  97.5 5.2 %collective-permute-start.2 = (f32[128,72]{0,1:T(8,128)S(1)}, f32[128,72]{0,1:T(8,128)S(1)}, u32[]{:S(2)}, u32[]{:S(2)}) collective-permute-start(f32[128,72]{0,1:T(8,128)S(1)} %collective-permute-done.1), channel_id=1, source_target_pairs={{0,1},{1,2},{2,3},{3,4},{4,5},{5,6},{6,7},{7,0},{8,9},{9,10},{10,1... | collective-permute-start | bytes 110600 | tf_op jit(solution)/shard_map/ppermute | solution.py:23
  97.8 6.4 %collective-permute-start.5 = (f32[128,72]{0,1:T(8,128)S(1)}, f32[128,72]{0,1:T(8,128)S(1)}, u32[]{:S(2)}, u32[]{:S(2)}) collective-permute-start(f32[128,72]{0,1:T(8,128)S(1)} %collective-permute-done.4), channel_id=1, source_target_pairs={{1,0},{2,1},{3,2},{4,3},{5,4},{6,5},{7,6},{0,7},{9,8},{10,9},{11,1... | collective-permute-start | bytes 110600 | tf_op jit(solution)/shard_map/ppermute | solution.py:25
  102.7 5.2 %collective-permute-start.3 = (f32[128,72]{0,1:T(8,128)S(1)}, f32[128,72]{0,1:T(8,128)S(1)}, u32[]{:S(2)}, u32[]{:S(2)}) collective-permute-start(f32[128,72]{0,1:T(8,128)S(1)} %collective-permute-done.2), channel_id=1, source_target_pairs={{0,1},{1,2},{2,3},{3,4},{4,5},{5,6},{6,7},{7,0},{8,9},{9,10},{10,1... | collective-permute-start | bytes 110600 | tf_op jit(solution)/shard_map/ppermute | solution.py:23
  104.2 5.2 %collective-permute-start.6 = (f32[128,72]{0,1:T(8,128)S(1)}, f32[128,72]{0,1:T(8,128)S(1)}, u32[]{:S(2)}, u32[]{:S(2)}) collective-permute-start(f32[128,72]{0,1:T(8,128)S(1)} %collective-permute-done.5), channel_id=1, source_target_pairs={{1,0},{2,1},{3,2},{4,3},{5,4},{6,5},{7,6},{0,7},{9,8},{10,9},{11,1... | collective-permute-start | bytes 110600 | tf_op jit(solution)/shard_map/ppermute | solution.py:25
Sparse Core Ops, SparseCore 0:
  28.9 33.1 reduce-scatter.2
  64.8 21.9 reduce-scatter.4
